TPU v7x, 16 devices: a whole 2x2x2 slice. The times are simulated.
16 devices in a mesh: data: 2 (over z), stage: 8 (over y, x, core).
Axes of the slice: x: 2, y: 2, z: 2, core: 2. Of those that a mesh axis runs over, the one named last changes fastest.
Arguments:
- X: bfloat16 [32, 256, 1024], P('data'), parts along dimension 0
- G: bfloat16 [32, 256, 1024], P('data'), parts along dimension 0
- W1: bfloat16 [8, 1024, 4096], P('stage')
- W2: bfloat16 [8, 4096, 1024], P('stage')
Outputs:
- output 1: bfloat16 [32, 256, 1024], P('data'), parts along dimension 0
- output 2: bfloat16 [32, 256, 1024], P('data'), parts along dimension 0
- output 3: float32 [16, 1024, 4096], P(('data', 'stage')), parts along dimension 0
- output 4: float32 [16, 4096, 1024], P(('data', 'stage')), parts along dimension 0
There are 2 independent parts. A program takes and returns all parts, laid end to end along the dimension named above; an argument that names none is the same for every part.
All inputs are finite; a program needn't handle non-finite values.
Results may differ from a plain program's by a relative error of at most 0.0134431.
Values are sent between devices in bfloat16 or wider.
A program may use at most 1 GiB of HBM per device.

v0:
```python
import jax
import jax.numpy as jnp
from jax import lax
from jax.sharding import PartitionSpec as P


def _fwd_layer(h, w1, w2):
    z = jnp.dot(h, w1, preferred_element_type=jnp.float32)
    u = jax.nn.gelu(z, approximate=True).astype(jnp.bfloat16)
    return (h.astype(jnp.float32) + jnp.dot(u, w2, preferred_element_type=jnp.float32)).astype(jnp.bfloat16)


def _bwd_layer(h, g, w1, w2):
    z = jnp.dot(h, w1, preferred_element_type=jnp.float32)
    u, gelu_vjp = jax.vjp(lambda t: jax.nn.gelu(t, approximate=True), z)
    du = jnp.dot(g, w2.T, preferred_element_type=jnp.float32)
    dz = gelu_vjp(du)[0].astype(jnp.bfloat16)
    dw2 = jnp.dot(u.astype(jnp.bfloat16).T, g, preferred_element_type=jnp.float32)
    dw1 = jnp.dot(h.T, dz, preferred_element_type=jnp.float32)
    dh = (g.astype(jnp.float32) + jnp.dot(dz, w1.T, preferred_element_type=jnp.float32)).astype(jnp.bfloat16)
    return dh, dw1, dw2


def _put(buf, i, val, ok):
    old = lax.dynamic_index_in_dim(buf, i, 0, keepdims=False)
    return lax.dynamic_update_index_in_dim(buf, jnp.where(ok, val, old), i, 0)


def solution(mesh):
    n_st = mesh.shape['stage']
    fwd_perm = [(i, i + 1) for i in range(n_st - 1)]
    bwd_perm = [(i + 1, i) for i in range(n_st - 1)]

    def body(x, g, w1, w2):
        s = lax.axis_index('stage')
        n_mb = x.shape[0]
        lps = w1.shape[0]
        first = s == 0
        last = s == n_st - 1
        ticks = n_mb + n_st - 1
        mb_shape = x.shape[1:]

        def fwd_tick(t, carry):
            recv, saved, y = carry
            m = t - s
            ok = (m >= 0) & (m < n_mb)
            mc = jnp.clip(m, 0, n_mb - 1)
            h = jnp.where(first, lax.dynamic_index_in_dim(x, mc, 0, keepdims=False), recv)
            hs = []
            for j in range(lps):
                hs.append(h)
                h = _fwd_layer(h, w1[j], w2[j])
            saved = _put(saved, mc, jnp.stack(hs), ok)
            y = _put(y, mc, h, ok & last)
            recv = lax.ppermute(h, 'stage', fwd_perm)
            return recv, saved, y

        recv0 = jnp.zeros(mb_shape, x.dtype)
        saved0 = jnp.zeros((n_mb, lps) + mb_shape, x.dtype)
        _, saved, y = lax.fori_loop(0, ticks, fwd_tick, (recv0, saved0, jnp.zeros_like(x)))

        def bwd_tick(t, carry):
            recv, dx, a1, a2 = carry
            m = t - (n_st - 1 - s)
            ok = (m >= 0) & (m < n_mb)
            mc = jnp.clip(m, 0, n_mb - 1)
            gh = jnp.where(last, lax.dynamic_index_in_dim(g, mc, 0, keepdims=False), recv)
            hs = lax.dynamic_index_in_dim(saved, mc, 0, keepdims=False)
            a1 = list(a1)
            a2 = list(a2)
            for j in reversed(range(lps)):
                gh, dw1, dw2 = _bwd_layer(hs[j], gh, w1[j], w2[j])
                a1[j] = a1[j] + jnp.where(ok, dw1, 0.0)
                a2[j] = a2[j] + jnp.where(ok, dw2, 0.0)
            dx = _put(dx, mc, gh, ok & first)
            recv = lax.ppermute(gh, 'stage', bwd_perm)
            return recv, dx, tuple(a1), tuple(a2)

        a10 = tuple(jnp.zeros(w1.shape[1:], jnp.float32) for _ in range(lps))
        a20 = tuple(jnp.zeros(w2.shape[1:], jnp.float32) for _ in range(lps))
        _, dx, a1, a2 = lax.fori_loop(0, ticks, bwd_tick, (recv0, jnp.zeros_like(x), a10, a20))
        y = lax.psum(y, 'stage')
        dx = lax.psum(dx, 'stage')
        return y, dx, jnp.stack(a1), jnp.stack(a2)

    return jax.shard_map(body, mesh=mesh,
                         in_specs=(P('data'), P('data'), P('stage'), P('stage')),
                         out_specs=(P('data'), P('data'), P(('data', 'stage')), P(('data', 'stage'))),
                         check_vma=False)
```

profile of v0, /device:TPU:0, one launch (start us, length us, event | category | flops | bytes accessed | tf_op | source)
XLA Modules:
  0.0 1989.4 jit_solution(12416894705016830510)
XLA Ops:
  16.2 542.2 %while.39 = (s32[]{:T(128)}, bf16[256,1024]{1,0:T(8,128)(2,1)S(1)}, bf16[16,1,256,1024]{3,2,1,0:T(8,128)(2,1)}, bf16[16,256,1024]{2,1,0:T(8,128)(2,1)}, pred[]{:...) while((s32[]{:T(128)}, bf16[256,1024]{1,0:T(8,128)(2,1)S(1)}, ...), condition=%wide.region_1.2_spmd, body=%wide.region_0.1_spmd.sunk | while | flops 4306501632 | bytes 27790580 | solution.py:60
  36.0 11.7 bitcast_dynamic-update-slice_fusion.6
  82.7 11.7 bitcast_dynamic-update-slice_fusion.6
  106.0 11.7 bitcast_dynamic-update-slice_fusion.6
  129.3 11.7 bitcast_dynamic-update-slice_fusion.6
  175.9 11.7 bitcast_dynamic-update-slice_fusion.6
  199.3 11.7 bitcast_dynamic-update-slice_fusion.6
  222.6 11.7 bitcast_dynamic-update-slice_fusion.6
  245.9 11.7 bitcast_dynamic-update-slice_fusion.6
  269.2 11.7 bitcast_dynamic-update-slice_fusion.6
  293.4 11.7 bitcast_dynamic-update-slice_fusion.6
  317.6 11.7 bitcast_dynamic-update-slice_fusion.6
  341.8 11.7 bitcast_dynamic-update-slice_fusion.6
  390.2 11.7 bitcast_dynamic-update-slice_fusion.6
  414.4 11.7 bitcast_dynamic-update-slice_fusion.6
  438.6 11.7 bitcast_dynamic-update-slice_fusion.6
  487.0 11.7 bitcast_dynamic-update-slice_fusion.6
  535.4 11.7 bitcast_dynamic-update-slice_fusion.6
  562.8 1161.0 %while.40 = (s32[]{:T(128)}, bf16[256,1024]{1,0:T(8,128)(2,1)S(1)}, bf16[16,256,1024]{2,1,0:T(8,128)(2,1)}, f32[1024,4096]{1,0:T(8,128)}, f32[4096,1024]{1,0:T(8...) while((s32[]{:T(128)}, bf16[256,1024]{1,0:T(8,128)(2,1)S(1)}, ...), condition=%wide.region_4.5_spmd.clone, body=%wide.region_3.4_spmd.clone.sunk | while | flops 10794303488 | bytes 162005360 | solution.py:81
  628.9 13.7 select_add_fusion.5
  642.6 14.5 select_add_fusion.4
  679.7 13.7 select_add_fusion.5
  693.4 14.5 select_add_fusion.4
  730.5 13.7 select_add_fusion.5
  744.2 14.5 select_add_fusion.4
  781.3 13.7 select_add_fusion.5
  795.0 14.5 select_add_fusion.4
  832.2 13.7 select_add_fusion.5
  845.9 14.5 select_add_fusion.4
  883.0 13.7 select_add_fusion.5
  896.7 14.5 select_add_fusion.4
  933.8 13.7 select_add_fusion.5
  947.5 14.5 select_add_fusion.4
  984.6 13.7 select_add_fusion.5
  998.3 14.5 select_add_fusion.4
  1035.4 13.7 select_add_fusion.5
  1049.1 14.5 select_add_fusion.4
  1086.2 13.7 select_add_fusion.5
  1099.9 14.5 select_add_fusion.4
  1136.9 13.7 select_add_fusion.5
  1150.6 14.5 select_add_fusion.4
  1187.7 13.7 select_add_fusion.5
  1201.4 14.5 select_add_fusion.4
  1238.5 13.7 select_add_fusion.5
  1252.2 14.5 select_add_fusion.4
  1289.3 13.7 select_add_fusion.5
  1303.0 14.5 select_add_fusion.4
  1340.0 13.7 select_add_fusion.5
  1353.7 14.5 select_add_fusion.4
  1390.8 13.7 select_add_fusion.5
  1404.5 14.5 select_add_fusion.4
  1441.6 13.7 select_add_fusion.5
  1455.3 14.5 select_add_fusion.4
  1492.4 13.7 select_add_fusion.5
  1506.1 14.5 select_add_fusion.4
  1543.2 13.7 select_add_fusion.5
  1556.9 14.5 select_add_fusion.4
  1594.0 13.7 select_add_fusion.5
  1607.7 14.5 select_add_fusion.4
  1644.7 13.7 select_add_fusion.5
  1658.5 14.5 select_add_fusion.4
  1695.6 13.7 select_add_fusion.5
  1709.3 14.5 select_add_fusion.4
  1723.8 242.5 %all-reduce.3.cloned.1.call-done = (bf16[16,256,1024]{2,1,0:T(8,128)(2,1)}, bf16[16,256,1024]{2,1,0:T(8,128)(2,1)}) async-done(((bf16[16,256,1024]{2,1,0:T(8,128)(2,1)}, bf16[16,256,1024]{2,1,0:T(8,128)(2,1)}), (bf16[16,256,1024]{2,1,0:T(8,128)(2,1)}, bf16[16,256,1024]{2,1,0:T(8,128)(2,1)})) %all-reduce.3.cloned.1.call-update) | async-done | bytes 16777232 | tf_op jit(solution)/shard_map/psum | solution.py:82
  (479 shorter events, 910.5 us)
Async XLA Ops:
  7.2 1959.1 %all-reduce.3.cloned.1.call-start = ((), (), s32[]{:S(2)}) async-start(), calls=%async_computation | async-start | bytes 33554432 | tf_op jit(solution)/shard_map/psum | solution.py:82
  29.0 5.9 collective-permute-start
  47.7 10.6 collective-permute-start
  71.1 10.5 collective-permute-start
  94.4 10.5 collective-permute-start
  117.7 10.4 collective-permute-start
  141.0 10.6 collective-permute-start
  164.4 10.4 collective-permute-start
  187.6 10.6 collective-permute-start
  211.0 10.5 collective-permute-start
  234.3 10.5 collective-permute-start
  257.6 10.5 collective-permute-start
  280.9 11.3 collective-permute-start
  305.1 11.4 collective-permute-start
  329.2 11.4 collective-permute-start
  353.5 11.4 collective-permute-start
  377.6 11.4 collective-permute-start
  401.8 11.4 collective-permute-start
  426.0 11.4 collective-permute-start
  450.2 11.4 collective-permute-start
  474.4 11.4 collective-permute-start
  498.6 11.4 collective-permute-start
  522.8 11.4 collective-permute-start
  547.0 11.4 collective-permute-start
  569.8 10.8 copy-start
  569.8 10.8 slice-start
  584.1 22.2 %collective-permute-start.1 = (bf16[256,1024]{1,0:T(8,128)(2,1)}, bf16[256,1024]{1,0:T(8,128)(2,1)S(1)}, u32[]{:S(2)}, u32[]{:S(2)}) collective-permute-start(bf16[256,1024]{1,0:T(8,128)(2,1)} %get-tuple-element.698), channel_id=1, source_target_pairs={{1,0},{2,1},{3,2},{4,3},{5,4},{6,5},{7,6},{9,8},{10,9},{11,10},{12... | collective-permute-start | bytes 1572872 | tf_op jit(solution)/shard_map/while/body/eval_jaxpr/ppermute | solution.py:76
  613.3 10.8 copy-start
  613.4 10.8 slice-start
  627.6 29.5 %collective-permute-start.1 = (bf16[256,1024]{1,0:T(8,128)(2,1)}, bf16[256,1024]{1,0:T(8,128)(2,1)S(1)}, u32[]{:S(2)}, u32[]{:S(2)}) collective-permute-start(bf16[256,1024]{1,0:T(8,128)(2,1)} %get-tuple-element.698), channel_id=1, source_target_pairs={{1,0},{2,1},{3,2},{4,3},{5,4},{6,5},{7,6},{9,8},{10,9},{11,10},{12... | collective-permute-start | bytes 1572872 | tf_op jit(solution)/shard_map/while/body/eval_jaxpr/ppermute | solution.py:76
  678.4 29.5 %collective-permute-start.1 = (bf16[256,1024]{1,0:T(8,128)(2,1)}, bf16[256,1024]{1,0:T(8,128)(2,1)S(1)}, u32[]{:S(2)}, u32[]{:S(2)}) collective-permute-start(bf16[256,1024]{1,0:T(8,128)(2,1)} %get-tuple-element.698), channel_id=1, source_target_pairs={{1,0},{2,1},{3,2},{4,3},{5,4},{6,5},{7,6},{9,8},{10,9},{11,10},{12... | collective-permute-start | bytes 1572872 | tf_op jit(solution)/shard_map/while/body/eval_jaxpr/ppermute | solution.py:76
  715.0 10.8 copy-start
  715.0 10.8 slice-start
  729.3 29.5 %collective-permute-start.1 = (bf16[256,1024]{1,0:T(8,128)(2,1)}, bf16[256,1024]{1,0:T(8,128)(2,1)S(1)}, u32[]{:S(2)}, u32[]{:S(2)}) collective-permute-start(bf16[256,1024]{1,0:T(8,128)(2,1)} %get-tuple-element.698), channel_id=1, source_target_pairs={{1,0},{2,1},{3,2},{4,3},{5,4},{6,5},{7,6},{9,8},{10,9},{11,10},{12... | collective-permute-start | bytes 1572872 | tf_op jit(solution)/shard_map/while/body/eval_jaxpr/ppermute | solution.py:76
  765.8 10.8 copy-start
  765.8 10.8 slice-start
  780.1 29.5 %collective-permute-start.1 = (bf16[256,1024]{1,0:T(8,128)(2,1)}, bf16[256,1024]{1,0:T(8,128)(2,1)S(1)}, u32[]{:S(2)}, u32[]{:S(2)}) collective-permute-start(bf16[256,1024]{1,0:T(8,128)(2,1)} %get-tuple-element.698), channel_id=1, source_target_pairs={{1,0},{2,1},{3,2},{4,3},{5,4},{6,5},{7,6},{9,8},{10,9},{11,10},{12... | collective-permute-start | bytes 1572872 | tf_op jit(solution)/shard_map/while/body/eval_jaxpr/ppermute | solution.py:76
  816.6 10.8 copy-start
  816.6 10.8 slice-start
  830.9 29.5 %collective-permute-start.1 = (bf16[256,1024]{1,0:T(8,128)(2,1)}, bf16[256,1024]{1,0:T(8,128)(2,1)S(1)}, u32[]{:S(2)}, u32[]{:S(2)}) collective-permute-start(bf16[256,1024]{1,0:T(8,128)(2,1)} %get-tuple-element.698), channel_id=1, source_target_pairs={{1,0},{2,1},{3,2},{4,3},{5,4},{6,5},{7,6},{9,8},{10,9},{11,10},{12... | collective-permute-start | bytes 1572872 | tf_op jit(solution)/shard_map/while/body/eval_jaxpr/ppermute | solution.py:76
  867.4 10.8 copy-start
  881.7 29.5 %collective-permute-start.1 = (bf16[256,1024]{1,0:T(8,128)(2,1)}, bf16[256,1024]{1,0:T(8,128)(2,1)S(1)}, u32[]{:S(2)}, u32[]{:S(2)}) collective-permute-start(bf16[256,1024]{1,0:T(8,128)(2,1)} %get-tuple-element.698), channel_id=1, source_target_pairs={{1,0},{2,1},{3,2},{4,3},{5,4},{6,5},{7,6},{9,8},{10,9},{11,10},{12... | collective-permute-start | bytes 1572872 | tf_op jit(solution)/shard_map/while/body/eval_jaxpr/ppermute | solution.py:76
  932.5 29.5 %collective-permute-start.1 = (bf16[256,1024]{1,0:T(8,128)(2,1)}, bf16[256,1024]{1,0:T(8,128)(2,1)S(1)}, u32[]{:S(2)}, u32[]{:S(2)}) collective-permute-start(bf16[256,1024]{1,0:T(8,128)(2,1)} %get-tuple-element.698), channel_id=1, source_target_pairs={{1,0},{2,1},{3,2},{4,3},{5,4},{6,5},{7,6},{9,8},{10,9},{11,10},{12... | collective-permute-start | bytes 1572872 | tf_op jit(solution)/shard_map/while/body/eval_jaxpr/ppermute | solution.py:76
  983.3 29.5 %collective-permute-start.1 = (bf16[256,1024]{1,0:T(8,128)(2,1)}, bf16[256,1024]{1,0:T(8,128)(2,1)S(1)}, u32[]{:S(2)}, u32[]{:S(2)}) collective-permute-start(bf16[256,1024]{1,0:T(8,128)(2,1)} %get-tuple-element.698), channel_id=1, source_target_pairs={{1,0},{2,1},{3,2},{4,3},{5,4},{6,5},{7,6},{9,8},{10,9},{11,10},{12... | collective-permute-start | bytes 1572872 | tf_op jit(solution)/shard_map/while/body/eval_jaxpr/ppermute | solution.py:76
  1019.8 10.8 copy-start
  1019.8 10.8 slice-start
  1034.1 29.5 %collective-permute-start.1 = (bf16[256,1024]{1,0:T(8,128)(2,1)}, bf16[256,1024]{1,0:T(8,128)(2,1)S(1)}, u32[]{:S(2)}, u32[]{:S(2)}) collective-permute-start(bf16[256,1024]{1,0:T(8,128)(2,1)} %get-tuple-element.698), channel_id=1, source_target_pairs={{1,0},{2,1},{3,2},{4,3},{5,4},{6,5},{7,6},{9,8},{10,9},{11,10},{12... | collective-permute-start | bytes 1572872 | tf_op jit(solution)/shard_map/while/body/eval_jaxpr/ppermute | solution.py:76
  1084.9 29.5 %collective-permute-start.1 = (bf16[256,1024]{1,0:T(8,128)(2,1)}, bf16[256,1024]{1,0:T(8,128)(2,1)S(1)}, u32[]{:S(2)}, u32[]{:S(2)}) collective-permute-start(bf16[256,1024]{1,0:T(8,128)(2,1)} %get-tuple-element.698), channel_id=1, source_target_pairs={{1,0},{2,1},{3,2},{4,3},{5,4},{6,5},{7,6},{9,8},{10,9},{11,10},{12... | collective-permute-start | bytes 1572872 | tf_op jit(solution)/shard_map/while/body/eval_jaxpr/ppermute | solution.py:76
  1121.4 10.8 copy-start
  1121.4 10.8 slice-start
  1135.7 29.5 %collective-permute-start.1 = (bf16[256,1024]{1,0:T(8,128)(2,1)}, bf16[256,1024]{1,0:T(8,128)(2,1)S(1)}, u32[]{:S(2)}, u32[]{:S(2)}) collective-permute-start(bf16[256,1024]{1,0:T(8,128)(2,1)} %get-tuple-element.698), channel_id=1, source_target_pairs={{1,0},{2,1},{3,2},{4,3},{5,4},{6,5},{7,6},{9,8},{10,9},{11,10},{12... | collective-permute-start | bytes 1572872 | tf_op jit(solution)/shard_map/while/body/eval_jaxpr/ppermute | solution.py:76
  1186.5 29.5 %collective-permute-start.1 = (bf16[256,1024]{1,0:T(8,128)(2,1)}, bf16[256,1024]{1,0:T(8,128)(2,1)S(1)}, u32[]{:S(2)}, u32[]{:S(2)}) collective-permute-start(bf16[256,1024]{1,0:T(8,128)(2,1)} %get-tuple-element.698), channel_id=1, source_target_pairs={{1,0},{2,1},{3,2},{4,3},{5,4},{6,5},{7,6},{9,8},{10,9},{11,10},{12... | collective-permute-start | bytes 1572872 | tf_op jit(solution)/shard_map/while/body/eval_jaxpr/ppermute | solution.py:76
  1237.2 29.5 %collective-permute-start.1 = (bf16[256,1024]{1,0:T(8,128)(2,1)}, bf16[256,1024]{1,0:T(8,128)(2,1)S(1)}, u32[]{:S(2)}, u32[]{:S(2)}) collective-permute-start(bf16[256,1024]{1,0:T(8,128)(2,1)} %get-tuple-element.698), channel_id=1, source_target_pairs={{1,0},{2,1},{3,2},{4,3},{5,4},{6,5},{7,6},{9,8},{10,9},{11,10},{12... | collective-permute-start | bytes 1572872 | tf_op jit(solution)/shard_map/while/body/eval_jaxpr/ppermute | solution.py:76
  1288.0 29.5 %collective-permute-start.1 = (bf16[256,1024]{1,0:T(8,128)(2,1)}, bf16[256,1024]{1,0:T(8,128)(2,1)S(1)}, u32[]{:S(2)}, u32[]{:S(2)}) collective-permute-start(bf16[256,1024]{1,0:T(8,128)(2,1)} %get-tuple-element.698), channel_id=1, source_target_pairs={{1,0},{2,1},{3,2},{4,3},{5,4},{6,5},{7,6},{9,8},{10,9},{11,10},{12... | collective-permute-start | bytes 1572872 | tf_op jit(solution)/shard_map/while/body/eval_jaxpr/ppermute | solution.py:76
  1338.7 29.5 %collective-permute-start.1 = (bf16[256,1024]{1,0:T(8,128)(2,1)}, bf16[256,1024]{1,0:T(8,128)(2,1)S(1)}, u32[]{:S(2)}, u32[]{:S(2)}) collective-permute-start(bf16[256,1024]{1,0:T(8,128)(2,1)} %get-tuple-element.698), channel_id=1, source_target_pairs={{1,0},{2,1},{3,2},{4,3},{5,4},{6,5},{7,6},{9,8},{10,9},{11,10},{12... | collective-permute-start | bytes 1572872 | tf_op jit(solution)/shard_map/while/body/eval_jaxpr/ppermute | solution.py:76
  1389.5 29.5 %collective-permute-start.1 = (bf16[256,1024]{1,0:T(8,128)(2,1)}, bf16[256,1024]{1,0:T(8,128)(2,1)S(1)}, u32[]{:S(2)}, u32[]{:S(2)}) collective-permute-start(bf16[256,1024]{1,0:T(8,128)(2,1)} %get-tuple-element.698), channel_id=1, source_target_pairs={{1,0},{2,1},{3,2},{4,3},{5,4},{6,5},{7,6},{9,8},{10,9},{11,10},{12... | collective-permute-start | bytes 1572872 | tf_op jit(solution)/shard_map/while/body/eval_jaxpr/ppermute | solution.py:76
  1440.3 29.5 %collective-permute-start.1 = (bf16[256,1024]{1,0:T(8,128)(2,1)}, bf16[256,1024]{1,0:T(8,128)(2,1)S(1)}, u32[]{:S(2)}, u32[]{:S(2)}) collective-permute-start(bf16[256,1024]{1,0:T(8,128)(2,1)} %get-tuple-element.698), channel_id=1, source_target_pairs={{1,0},{2,1},{3,2},{4,3},{5,4},{6,5},{7,6},{9,8},{10,9},{11,10},{12... | collective-permute-start | bytes 1572872 | tf_op jit(solution)/shard_map/while/body/eval_jaxpr/ppermute | solution.py:76
  1491.1 29.5 %collective-permute-start.1 = (bf16[256,1024]{1,0:T(8,128)(2,1)}, bf16[256,1024]{1,0:T(8,128)(2,1)S(1)}, u32[]{:S(2)}, u32[]{:S(2)}) collective-permute-start(bf16[256,1024]{1,0:T(8,128)(2,1)} %get-tuple-element.698), channel_id=1, source_target_pairs={{1,0},{2,1},{3,2},{4,3},{5,4},{6,5},{7,6},{9,8},{10,9},{11,10},{12... | collective-permute-start | bytes 1572872 | tf_op jit(solution)/shard_map/while/body/eval_jaxpr/ppermute | solution.py:76
  1541.9 29.5 %collective-permute-start.1 = (bf16[256,1024]{1,0:T(8,128)(2,1)}, bf16[256,1024]{1,0:T(8,128)(2,1)S(1)}, u32[]{:S(2)}, u32[]{:S(2)}) collective-permute-start(bf16[256,1024]{1,0:T(8,128)(2,1)} %get-tuple-element.698), channel_id=1, source_target_pairs={{1,0},{2,1},{3,2},{4,3},{5,4},{6,5},{7,6},{9,8},{10,9},{11,10},{12... | collective-permute-start | bytes 1572872 | tf_op jit(solution)/shard_map/while/body/eval_jaxpr/ppermute | solution.py:76
  1592.7 29.5 %collective-permute-start.1 = (bf16[256,1024]{1,0:T(8,128)(2,1)}, bf16[256,1024]{1,0:T(8,128)(2,1)S(1)}, u32[]{:S(2)}, u32[]{:S(2)}) collective-permute-start(bf16[256,1024]{1,0:T(8,128)(2,1)} %get-tuple-element.698), channel_id=1, source_target_pairs={{1,0},{2,1},{3,2},{4,3},{5,4},{6,5},{7,6},{9,8},{10,9},{11,10},{12... | collective-permute-start | bytes 1572872 | tf_op jit(solution)/shard_map/while/body/eval_jaxpr/ppermute | solution.py:76
  1643.5 29.5 %collective-permute-start.1 = (bf16[256,1024]{1,0:T(8,128)(2,1)}, bf16[256,1024]{1,0:T(8,128)(2,1)S(1)}, u32[]{:S(2)}, u32[]{:S(2)}) collective-permute-start(bf16[256,1024]{1,0:T(8,128)(2,1)} %get-tuple-element.698), channel_id=1, source_target_pairs={{1,0},{2,1},{3,2},{4,3},{5,4},{6,5},{7,6},{9,8},{10,9},{11,10},{12... | collective-permute-start | bytes 1572872 | tf_op jit(solution)/shard_map/while/body/eval_jaxpr/ppermute | solution.py:76
  1680.0 10.8 copy-start
  1680.0 10.8 slice-start
  1694.3 29.5 %collective-permute-start.1 = (bf16[256,1024]{1,0:T(8,128)(2,1)}, bf16[256,1024]{1,0:T(8,128)(2,1)S(1)}, u32[]{:S(2)}, u32[]{:S(2)}) collective-permute-start(bf16[256,1024]{1,0:T(8,128)(2,1)} %get-tuple-element.698), channel_id=1, source_target_pairs={{1,0},{2,1},{3,2},{4,3},{5,4},{6,5},{7,6},{9,8},{10,9},{11,10},{12... | collective-permute-start | bytes 1572872 | tf_op jit(solution)/shard_map/while/body/eval_jaxpr/ppermute | solution.py:76
  (52 other events, 521.5 us)
Sparse Core Ops, SparseCore 0:
  1723.9 242.2 all-reduce.2
where the time goes:
time: 2000 us; the launch traced here: 1990 us
  matrix products  1330 us (66%)
  waiting for transfers between devices  243 us (12%)
  starting transfers between devices  203 us (10%)
  local copies, waits for them, and re-layouts  105 us (5%)
  other arithmetic  86.1 us (4%)
    dot_general x23, matrix products, _bwd_layer(): dw1 = jnp.dot(h.T, dz, preferred_element_type=jnp.float32)  329 us
    dot_general x23, matrix products, _bwd_layer(): jnp.dot(u.astype(jnp.bfloat16).T, g, preferred_element_type=jnp.float32)  313 us
    dot_general x23, matrix products, _fwd_layer(): jnp.dot(u, w2, preferred_element_type=jnp.float32)  268 us
    psum x1, waiting for transfers between devices, body(): y = lax.psum(y, 'stage')  242 us
    dot_general x23, matrix products, _bwd_layer(): du = jnp.dot(g, w2.T, preferred_element_type=jnp.float32)  209 us
    ppermute x23, starting transfers between devices, fwd_tick(): recv = lax.ppermute(h, 'stage', fwd_perm)  174 us
    dot_general x23, matrix products, _bwd_layer(): z = jnp.dot(h, w1, preferred_element_type=jnp.float32)  136 us
    dot_general x23, matrix products, _bwd_layer(): jnp.dot(dz, w1.T, preferred_element_type=jnp.float32)  80.3 us
  transfers between devices with their start and end apart: 47, of which 1 were waited for; matrix products, arithmetic and copies ran while one was open for 36% of the time, Pallas kernels for 0%

commit v1 on v0

v1 whole, which is shorter than its diff:
```python
import functools

import jax
import jax.numpy as jnp
from jax import lax
from jax.experimental import pallas as pl
from jax.experimental.pallas import tpu as pltpu
from jax.sharding import PartitionSpec as P

BF = jnp.bfloat16
F32 = jnp.float32
C0 = 0.7978845608028654
C1 = 0.044715
NT = (((1,), (1,)), ((), ()))
FT = 512
OT = 512
WARM = (16, 16, 16, 16, 10, 8, 3, 1)
LAG_Y = (0, 3, 0, 2, 0, 1, 0, 0)
LAG_X = (0, 0, 4, 0, 4, 0, 8, 0)


def _gelu(z):
    a = (C0 * C1) * (z * z)
    s = 0.5 * jnp.tanh(z * (a + C0)) + 0.5
    u = z * s
    return u, s + (u - u * s) * (6.0 * a + 2.0 * C0)


def _pick(s, table):
    out = jnp.int32(table[-1])
    for i, v in enumerate(table[:-1]):
        out = jnp.where(s == i, jnp.int32(v), out)
    return out


def _pipe(n, n_st, x, gin, w1h, w2h, y, dx, hs, gs, us, dzs, gps,
          w1, w2, h_all, g_all, u, gp, dz, of, ob,
          w_sem, h_recv, g_recv, y_recv, x_recv, hs_sem, gs_sem,
          u_sem, gp_sem, pf_sem, dz_sem, f_send, b_send,
          y_loc, y_send, x_loc, x_send, yr_send, xr_send):
    s = lax.axis_index('stage')
    first = s == 0
    last = s == n_st - 1
    w = _pick(s, WARM)
    lag_y = _pick(s, LAG_Y)
    lag_x = _pick(s, LAG_X)
    f_dim = w1.shape[1]
    d_dim = w1.shape[0]

    def local(src, dst, sem):
        return pltpu.make_async_copy(src, dst, sem)

    def remote(src, dst, ssem, rsem, dev):
        return pltpu.make_async_remote_copy(
            src_ref=src, dst_ref=dst, send_sem=ssem, recv_sem=rsem,
            device_id={'stage': dev}, device_id_type=pl.DeviceIdType.MESH)

    @pl.when(first)
    def _():
        local(x.at[0], h_all.at[0], h_recv.at[0]).start()
    local(w1h, w1, w_sem.at[0]).start()
    local(w2h, w2, w_sem.at[1]).start()

    @pl.when(first)
    def _():
        def go(m, c):
            local(x.at[m], h_all.at[m], h_recv.at[m]).start()
            return c
        lax.fori_loop(1, n, go, 0)

    @pl.when(last)
    def _():
        def go(m, c):
            local(gin.at[m], g_all.at[m], g_recv.at[m]).start()
            return c
        lax.fori_loop(0, n, go, 0)
    local(w1h, w1, w_sem.at[0]).wait()
    local(w2h, w2, w_sem.at[1]).wait()

    relay_y = (s == 1) | (s == 3) | (s == 5)
    relay_x = (s == 2) | (s == 4) | (s == 6)

    def pass_y(m):
        local(y.at[m], y.at[m], y_recv.at[m]).wait()

        @pl.when(relay_y)
        def _():
            remote(y.at[m], y.at[m], yr_send.at[0, m], y_recv.at[m], s - 1).start()

        @pl.when(s == 5)
        def _():
            remote(y.at[m], y.at[m], yr_send.at[1, m], y_recv.at[m], 1).start()

    def pass_x(m):
        local(dx.at[m], dx.at[m], x_recv.at[m]).wait()

        @pl.when(relay_x)
        def _():
            remote(dx.at[m], dx.at[m], xr_send.at[0, m], x_recv.at[m], s + 1).start()

        @pl.when(s == 2)
        def _():
            remote(dx.at[m], dx.at[m], xr_send.at[1, m], x_recv.at[m], 6).start()

    def wait_f_send(sl):
        @pl.when(last)
        def _():
            local(of.at[sl], y.at[0], y_loc.at[sl]).wait()
            for k, dev in enumerate((6, 5, 3)):
                remote(of.at[sl], y.at[0], y_send.at[k, sl], y_recv.at[0], dev).wait_send()

        @pl.when(jnp.logical_not(last))
        def _():
            remote(of.at[sl], h_all.at[0], f_send.at[sl], h_recv.at[0], s + 1).wait_send()

    def wait_b_send(sl):
        @pl.when(first)
        def _():
            local(ob.at[sl], dx.at[0], x_loc.at[sl]).wait()
            for k, dev in enumerate((1, 2, 4)):
                remote(ob.at[sl], dx.at[0], x_send.at[k, sl], x_recv.at[0], dev).wait_send()

        @pl.when(jnp.logical_not(first))
        def _():
            remote(ob.at[sl], g_all.at[0], b_send.at[sl], g_recv.at[0], s - 1).wait_send()

    def wait_f_store(sl):
        local(u.at[sl], us.at[0], u_sem.at[sl]).wait()
        local(gp.at[sl], gps.at[0], gp_sem.at[sl]).wait()

    def forward(m):
        sl = m % 2
        local(h_all.at[m], h_all.at[m], h_recv.at[m]).wait()
        local(h_all.at[m], hs.at[m], hs_sem).start()

        @pl.when(m >= 2)
        def _():
            wait_f_send(sl)
        h = h_all.at[m]
        for j in range(f_dim // FT):
            c = pl.ds(j * FT, FT)
            z = jnp.dot(h[...], w1[:, c], preferred_element_type=F32)
            uu, gg = _gelu(z)
            u[sl, :, c] = uu.astype(BF)
            gp[sl, :, c] = gg
        for j in range(d_dim // OT):
            c = pl.ds(j * OT, OT)
            r = jnp.dot(u[sl], w2[:, c], preferred_element_type=F32)
            of[sl, :, c] = (h[:, c].astype(F32) + r).astype(BF)

        @pl.when(last)
        def _():
            for k, dev in enumerate((6, 5, 3)):
                remote(of.at[sl], y.at[m], y_send.at[k, sl], y_recv.at[m], dev).start()
            local(of.at[sl], y.at[m], y_loc.at[sl]).start()

        @pl.when(jnp.logical_not(last))
        def _():
            remote(of.at[sl], h_all.at[m], f_send.at[sl], h_recv.at[m], s + 1).start()
        local(u.at[sl], us.at[m], u_sem.at[sl]).start()
        local(gp.at[sl], gps.at[m], gp_sem.at[sl]).start()

    def backward(m):
        sl = m % 2
        gi = jnp.where(w == 1, sl, 2)
        local(g_all.at[m], g_all.at[m], g_recv.at[m]).wait()
        local(g_all.at[m], gs.at[m], gs_sem).start()

        @pl.when(w > 1)
        def _():
            local(gps.at[m], gp.at[2], pf_sem).wait()

        @pl.when(m >= 2)
        def _():
            wait_b_send(sl)
            local(dz.at[sl], dzs.at[0], dz_sem.at[sl]).wait()
        g = g_all.at[m]
        for j in range(f_dim // FT):
            c = pl.ds(j * FT, FT)
            du = lax.dot_general(g[...], w2[c, :], NT, preferred_element_type=F32)
            dz[sl, :, c] = (gp[gi, :, c] * du).astype(BF)
        for j in range(d_dim // OT):
            c = pl.ds(j * OT, OT)
            r = lax.dot_general(dz[sl], w1[c, :], NT, preferred_element_type=F32)
            ob[sl, :, c] = (g[:, c].astype(F32) + r).astype(BF)

        @pl.when(first)
        def _():
            for k, dev in enumerate((1, 2, 4)):
                remote(ob.at[sl], dx.at[m], x_send.at[k, sl], x_recv.at[m], dev).start()
            local(ob.at[sl], dx.at[m], x_loc.at[sl]).start()

        @pl.when(jnp.logical_not(first))
        def _():
            remote(ob.at[sl], g_all.at[m], b_send.at[sl], g_recv.at[m], s - 1).start()
        local(dz.at[sl], dzs.at[m], dz_sem.at[sl]).start()

    ticks = n + jnp.maximum(w, 2)

    def tick(t, c):
        @pl.when((t >= 2) & (t < n + 2))
        def _():
            wait_f_store(t % 2)

        @pl.when((t >= w) & (t - w < n))
        def _():
            backward(t - w)

        @pl.when((w > 1) & (t - w + 1 >= 0) & (t - w + 1 < n))
        def _():
            local(gps.at[t - w + 1], gp.at[2], pf_sem).start()

        @pl.when(t < n)
        def _():
            forward(t)

        my = t - w - lag_y

        @pl.when(relay_y & (my >= 0) & (my < n))
        def _():
            pass_y(my)
        mx = t - w - lag_x

        @pl.when(relay_x & (mx >= 0) & (mx < n))
        def _():
            pass_x(mx)
        return c
    lax.fori_loop(0, ticks, tick, 0)

    y0 = jnp.where(relay_y, jnp.clip(ticks - w - lag_y, 0, n), jnp.where(last, n, 0))
    x0 = jnp.where(relay_x, jnp.clip(ticks - w - lag_x, 0, n), jnp.where(first, n, 0))

    def rest_y(m, c):
        pass_y(m)
        return c

    def rest_x(m, c):
        pass_x(m)
        return c
    lax.fori_loop(y0, n, rest_y, 0)
    lax.fori_loop(x0, n, rest_x, 0)
    for m in (n - 2, n - 1):
        wait_f_send(m % 2)
        wait_b_send(m % 2)
        local(dz.at[m % 2], dzs.at[0], dz_sem.at[m % 2]).wait()
    local(h_all, hs, hs_sem).wait()
    local(g_all, gs, gs_sem).wait()

    def done(m, c):
        @pl.when(relay_y)
        def _():
            remote(y.at[m], y.at[m], yr_send.at[0, m], y_recv.at[m], s - 1).wait_send()

        @pl.when(s == 5)
        def _():
            remote(y.at[m], y.at[m], yr_send.at[1, m], y_recv.at[m], 1).wait_send()

        @pl.when(relay_x)
        def _():
            remote(dx.at[m], dx.at[m], xr_send.at[0, m], x_recv.at[m], s + 1).wait_send()

        @pl.when(s == 2)
        def _():
            remote(dx.at[m], dx.at[m], xr_send.at[1, m], x_recv.at[m], 6).wait_send()
        return c
    lax.fori_loop(0, n, done, 0)


def _run_pipe(n_st, x, g, w1, w2):
    n, b, d = x.shape
    f = w1.shape[1]
    act = jax.ShapeDtypeStruct((n, b, d), BF)
    wide = jax.ShapeDtypeStruct((n, b, f), BF)
    anyspec = pl.BlockSpec(memory_space=pl.ANY)
    dma = pltpu.SemaphoreType.DMA
    return pl.pallas_call(
        functools.partial(_pipe, n, n_st),
        out_shape=(act, act, act, act, wide, wide, jax.ShapeDtypeStruct((n, b, f), F32)),
        in_specs=[anyspec] * 4,
        out_specs=(anyspec,) * 7,
        scratch_shapes=[
            pltpu.VMEM((d, f), BF), pltpu.VMEM((f, d), BF),
            pltpu.VMEM((n, b, d), BF), pltpu.VMEM((n, b, d), BF),
            pltpu.VMEM((2, b, f), BF), pltpu.VMEM((3, b, f), F32), pltpu.VMEM((2, b, f), BF),
            pltpu.VMEM((2, b, d), BF), pltpu.VMEM((2, b, d), BF),
            dma((2,)), dma((n,)), dma((n,)), dma((n,)), dma((n,)), dma, dma,
            dma((2,)), dma((2,)), dma, dma((2,)), dma((2,)), dma((2,)),
            dma((2,)), dma((3, 2)), dma((2,)), dma((3, 2)), dma((2, n)), dma((2, n)),
        ],
        compiler_params=pltpu.CompilerParams(has_side_effects=True, vmem_limit_bytes=63 * 1024 * 1024),
    )(x, g, w1, w2)


def solution(mesh):
    n_st = mesh.shape['stage']

    def body(x, g, w1, w2):
        n, b, d = x.shape
        f = w1.shape[2]
        y, dx, hs, gs, us, dzs, _ = _run_pipe(n_st, x, g, w1[0], w2[0])
        tn = (((0,), (0,)), ((), ()))
        hs, gs = hs.reshape(n * b, d), gs.reshape(n * b, d)
        us, dzs = us.reshape(n * b, f), dzs.reshape(n * b, f)
        dw1 = lax.dot_general(hs, dzs, tn, preferred_element_type=F32)
        dw2 = lax.dot_general(us, gs, tn, preferred_element_type=F32)
        return y, dx, dw1[None], dw2[None]

    return jax.shard_map(body, mesh=mesh,
                         in_specs=(P('data'), P('data'), P('stage'), P('stage')),
                         out_specs=(P('data'), P('data'), P(('data', 'stage')), P(('data', 'stage'))),
                         check_vma=False)
```

time: 2000 us -> 447 us (0.22)
  the two profiles are of different devices: /device:TPU:0 before, /device:TPU:15 now
where the time goes in v1:
time: 447 us
  Pallas kernels  344 us (77%)
  matrix products  85.9 us (19%)
  local copies, waits for them, and re-layouts  16.2 us (4%)
    pallas_call x1, Pallas kernels, _run_pipe(): pl.pallas_call(functools.partial(_pipe, n, n_st), out_shape=(act, act, ac...  344 us
    dot_general x1, matrix products, body(): dw1 = lax.dot_general(hs, dzs, tn, preferred_element_type=F32)  43.8 us
    dot_general x1, matrix products, body(): dw2 = lax.dot_general(us, gs, tn, preferred_element_type=F32)  42.1 us
    unnamed x4, local copies, waits for them, and re-layouts  16.2 us

profile of v1, /device:TPU:15, one launch (start us, length us, event | category | flops | bytes accessed | tf_op | source)
XLA Modules:
  0.0 447.2 jit_solution(14019710164212253359)
XLA Ops:
  0.6 344.5 %shard_map.75 = (bf16[16,256,1024]{2,1,0:T(8,128)(2,1)}, bf16[16,256,1024]{2,1,0:T(8,128)(2,1)}, bf16[16,256,1024]{2,1,0:T(8,128)(2,1)}, bf16[16,256,1024]{2,1,0...) custom-call(bf16[16,256,1024]{2,1,0:T(8,128)(2,1)} %x.1, ...), custom_call_target="tpu_custom_call" | custom-call | tf_op jit(solution)/shard_map/pallas_call | solution.py:276
  345.1 0.0 copy-start
  345.1 43.8 %convolution_bitcast_fusion.1 = f32[1,1024,4096]{2,1,0:T(8,128)} fusion(bf16[16,256,1024]{2,1,0:T(8,128)(2,1)} %get-tuple-element.12, bf16[16,256,4096]{2,1,0:T(8,128)(2,1)} %get-tuple-element.13), kind=kOutput, calls=%fused_computation.1 | convolution fusion | flops 34359738368 | bytes 58720256 | tf_op jit(solution)/shard_map/dot_general | solution.py:304
  388.9 0.0 copy-done
  388.9 42.1 %convolution_bitcast_fusion = f32[1,4096,1024]{2,1,0:T(8,128)} fusion(bf16[16,256,4096]{2,1,0:T(8,128)(2,1)} %get-tuple-element.14, bf16[16,256,1024]{2,1,0:T(8,128)(2,1)S(1)} %copy-done), kind=kOutput, calls=%fused_computation | convolution fusion | flops 34359738368 | bytes 58720256 | tf_op jit(solution)/shard_map/dot_general | solution.py:305
  431.0 8.1 %copy.14 = bf16[16,256,1024]{2,1,0:T(8,128)(2,1)} copy(bf16[16,256,1024]{2,1,0:T(8,128)(2,1)} %get-tuple-element.20) | data formatting | bytes 16777216
  439.1 8.1 %copy.15 = bf16[16,256,1024]{2,1,0:T(8,128)(2,1)} copy(bf16[16,256,1024]{2,1,0:T(8,128)(2,1)} %get-tuple-element.21) | data formatting | bytes 16777216
Async XLA Ops:
  345.1 43.8 %copy-start = (bf16[16,256,1024]{2,1,0:T(8,128)(2,1)S(1)}, bf16[16,256,1024]{2,1,0:T(8,128)(2,1)}, u32[]{:S(2)}) copy-start(bf16[16,256,1024]{2,1,0:T(8,128)(2,1)} %get-tuple-element.15) | copy-start | bytes 25165828

commit v2 on v1

v2 whole, which is shorter than its diff:
```python
import functools

import jax
import jax.numpy as jnp
from jax import lax
from jax.experimental import pallas as pl
from jax.experimental.pallas import tpu as pltpu
from jax.sharding import PartitionSpec as P

BF = jnp.bfloat16
F32 = jnp.float32
C0 = 0.7978845608028654
C1 = 0.044715
NT = (((1,), (1,)), ((), ()))
TN = (((0,), (0,)), ((), ()))
FT = 512
OT = 512
WARM = (16, 16, 16, 16, 11, 9, 3, 1)
KB = 8
PAR_Y = (0, 0, 0, 1, 0, 0, 0, 0)
OFF_P = (99, 17, 99, 16, 99, 14, 99, 99)
OFF_S = (99, 17, 99, 22, 99, 21, 99, 99)
LAG_X = (0, 0, 5, 0, 7, 0, 12, 0)
NF = 4
T_W = (25, 25, 28, 32, 27, 25, 19, 18)
YC = 12
LATE_Y = {20: 12, 21: 14, 23: 13, 24: 15}


def _gelu(z):
    a = (C0 * C1) * (z * z)
    s = 0.5 * jnp.tanh(z * (a + C0)) + 0.5
    u = z * s
    return u, s + (u - u * s) * (6.0 * a + 2.0 * C0)


def _pick(s, table):
    out = jnp.int32(table[-1])
    for i, v in enumerate(table[:-1]):
        out = jnp.where(s == i, jnp.int32(v), out)
    return out


def _pipe(n, n_st, x, gin, w1h, w2h, y, dx, hs, gs, us, dzs, gps, p1, p2,
          w1, w2, h_all, g_all, u, gp, dz, of, ob,
          w_sem, h_recv, g_recv, y_recv, x_recv, hs_sem, gs_sem,
          u_sem, gp_sem, pf_sem, dz_sem, f_send, b_send,
          y_loc, y_send, x_loc, x_send, yr_send, xr_send, wu_sem, wd_sem, wo_sem):
    s = lax.axis_index('stage')
    first = s == 0
    last = s == n_st - 1
    w = _pick(s, WARM)
    par_y = _pick(s, PAR_Y)
    off_p = _pick(s, OFF_P)
    off_s = _pick(s, OFF_S)
    lag_x = _pick(s, LAG_X)
    f_dim = w1.shape[1]
    d_dim = w1.shape[0]

    def local(src, dst, sem):
        return pltpu.make_async_copy(src, dst, sem)

    def remote(src, dst, ssem, rsem, dev):
        return pltpu.make_async_remote_copy(
            src_ref=src, dst_ref=dst, send_sem=ssem, recv_sem=rsem,
            device_id={'stage': dev}, device_id_type=pl.DeviceIdType.MESH)

    @pl.when(first)
    def _():
        local(x.at[0], h_all.at[0], h_recv.at[0]).start()
    local(w1h, w1, w_sem.at[0]).start()
    local(w2h, w2, w_sem.at[1]).start()

    @pl.when(last)
    def _():
        def go(m, c):
            local(gin.at[m], g_all.at[m], g_recv.at[m]).start()
            return c
        lax.fori_loop(0, n, go, 0)
    local(w1h, w1, w_sem.at[0]).wait()
    local(w2h, w2, w_sem.at[1]).wait()

    @pl.when(first)
    def _():
        def go(m, c):
            local(x.at[m], h_all.at[m], h_recv.at[m]).start()
            return c
        lax.fori_loop(1, n, go, 0)

    relay_y = (s == 1) | (s == 3) | (s == 5)
    relay_x = (s == 2) | (s == 4) | (s == 6)

    def second_y(m):
        return (s == 1) | ((s == 5) & (m % 2 == 0)) | ((s == 3) & (m % 2 == 1))

    def next_y(m):
        return jnp.where(s == 1, 3 + 2 * (m % 2), 1)

    def pass_y(m):
        local(y.at[m], y.at[m], y_recv.at[m]).wait()

        @pl.when(relay_y)
        def _():
            remote(y.at[m], y.at[m], yr_send.at[0, m], y_recv.at[m], s - 1).start()

        @pl.when(second_y(m))
        def _():
            remote(y.at[m], y.at[m], yr_send.at[1, m], y_recv.at[m], next_y(m)).start()

    def pass_x(m):
        local(dx.at[m], dx.at[m], x_recv.at[m]).wait()

        @pl.when(relay_x)
        def _():
            remote(dx.at[m], dx.at[m], xr_send.at[0, m], x_recv.at[m], s + 1).start()

        @pl.when(s == 2)
        def _():
            remote(dx.at[m], dx.at[m], xr_send.at[1, m], x_recv.at[m], 6).start()

    def wait_f_send(sl):
        remote(of.at[sl], h_all.at[0], f_send.at[sl], h_recv.at[0], s + 1).wait_send()

    def wait_b_send(sl):
        @pl.when(first)
        def _():
            local(ob.at[sl], dx.at[0], x_loc.at[sl]).wait()
            for k, dev in enumerate((1, 2, 4)):
                remote(ob.at[sl], dx.at[0], x_send.at[k, sl], x_recv.at[0], dev).wait_send()

        @pl.when(jnp.logical_not(first))
        def _():
            remote(ob.at[sl], g_all.at[0], b_send.at[sl], g_recv.at[0], s - 1).wait_send()

    def wait_f_store(sl):
        local(u.at[sl], us.at[0], u_sem.at[sl]).wait()
        local(gp.at[sl], gps.at[0], gp_sem.at[sl]).wait()

    def forward(m):
        sl = m % NF
        su = m % 2
        local(h_all.at[m], h_all.at[m], h_recv.at[m]).wait()
        local(h_all.at[m], hs.at[m], hs_sem).start()

        @pl.when(jnp.logical_not(last) & (m >= NF))
        def _():
            wait_f_send(sl)
        h = h_all.at[m]
        with jax.named_scope('F'):
            for j in range(f_dim // FT):
                c = pl.ds(j * FT, FT)
                z = jnp.dot(h[...], w1[:, c], preferred_element_type=F32)
                uu, gg = _gelu(z)
                u[su, :, c] = uu.astype(BF)
                gp[su, :, c] = gg
            for j in range(d_dim // OT):
                c = pl.ds(j * OT, OT)
                r = jnp.dot(u[su], w2[:, c], preferred_element_type=F32)
                of[sl, :, c] = (h[:, c].astype(F32) + r).astype(BF)

        @pl.when(last)
        def _():
            local(of.at[sl], y.at[m], y_loc.at[sl]).start()

        @pl.when(jnp.logical_not(last))
        def _():
            remote(of.at[sl], h_all.at[m], f_send.at[sl], h_recv.at[m], s + 1).start()
        local(u.at[su], us.at[m], u_sem.at[su]).start()
        local(gp.at[su], gps.at[m], gp_sem.at[su]).start()

    def backward(m):
        sl = m % 2
        gi = jnp.where(w == 1, sl, 2)
        local(g_all.at[m], g_all.at[m], g_recv.at[m]).wait()
        local(g_all.at[m], gs.at[m], gs_sem).start()

        @pl.when(w > 1)
        def _():
            local(gps.at[m], gp.at[2], pf_sem).wait()

        @pl.when(m >= 2)
        def _():
            wait_b_send(sl)

        @pl.when(m >= 1)
        def _():
            local(dz, dzs.at[0], dz_sem).wait()
        g = g_all.at[m]
        with jax.named_scope('B'):
            for j in range(f_dim // FT):
                c = pl.ds(j * FT, FT)
                du = lax.dot_general(g[...], w2[c, :], NT, preferred_element_type=F32)
                dz[:, c] = (gp[gi, :, c] * du).astype(BF)
            local(dz, dzs.at[m], dz_sem).start()
            for j in range(d_dim // OT):
                c = pl.ds(j * OT, OT)
                r = lax.dot_general(dz[...], w1[c, :], NT, preferred_element_type=F32)
                ob[sl, :, c] = (g[:, c].astype(F32) + r).astype(BF)

        @pl.when(first)
        def _():
            for k, dev in enumerate((1, 2, 4)):
                remote(ob.at[sl], dx.at[m], x_send.at[k, sl], x_recv.at[m], dev).start()
            local(ob.at[sl], dx.at[m], x_loc.at[sl]).start()

        @pl.when(jnp.logical_not(first))
        def _():
            remote(ob.at[sl], g_all.at[m], b_send.at[sl], g_recv.at[m], s - 1).start()

    n_grp = f_dim // FT

    def w_load(i):
        c = pl.ds(pl.multiple_of(i * FT, FT), FT)
        sl = i % 2
        for k in range(KB):
            to = pl.ds(k * FT, FT)
            local(us.at[k, :, c], u.at[2 * sl, :, to], wu_sem.at[sl]).start()
            local(dzs.at[k, :, c], u.at[2 * sl + 1, :, to], wd_sem.at[sl]).start()

    def w_group(i):
        sl = i % 2

        @pl.when(i + 1 < n_grp)
        def _():
            w_load(i + 1)
        local(us.at[0], u.at[2 * sl], wu_sem.at[sl]).wait()
        local(dzs.at[0], u.at[2 * sl + 1], wd_sem.at[sl]).wait()

        @pl.when(i >= 2)
        def _():
            local(gp.at[sl], gps.at[0], wo_sem.at[sl]).wait()
        kt = KB * h_all.shape[1]
        b = h_all.shape[1]
        with jax.named_scope('W'):
            lhs = jnp.concatenate([u[2 * sl, :, k * FT:(k + 1) * FT] for k in range(KB)], axis=0)
            r = lax.dot_general(lhs, g_all[0:KB].reshape(kt, d_dim), TN, preferred_element_type=F32)
            for q in range(FT // b):
                gp[sl, :, d_dim * q:d_dim * (q + 1)] = r[b * q:b * (q + 1)]
            rhs = jnp.concatenate([u[2 * sl + 1, :, k * FT:(k + 1) * FT] for k in range(KB)], axis=0)
            r = lax.dot_general(h_all[0:KB].reshape(kt, d_dim), rhs, TN, preferred_element_type=F32)
            for q in range(d_dim // b):
                gp[sl, :, 2 * d_dim + FT * q:2 * d_dim + FT * (q + 1)] = r[b * q:b * (q + 1)]
        for q in range(FT // b):
            local(gp.at[sl, :, pl.ds(d_dim * q, d_dim)],
                  p2.at[pl.ds(pl.multiple_of(i * FT + b * q, b), b), :], wo_sem.at[sl]).start()
        for q in range(d_dim // b):
            local(gp.at[sl, :, pl.ds(2 * d_dim + FT * q, FT)],
                  p1.at[pl.ds(b * q, b), pl.ds(pl.multiple_of(i * FT, FT), FT)], wo_sem.at[sl]).start()

    t0 = _pick(s, T_W)
    ticks = jnp.maximum(jnp.maximum(n + w, t0 + n_grp), n + 2)

    def send_y(m):
        remote(y.at[m], y.at[m], y_send.at[0, m], y_recv.at[m], 6).start()
        remote(y.at[m], y.at[m], y_send.at[1, m], y_recv.at[m], 5 - 2 * (m % 2)).start()

    def tick(t, c):
        @pl.when((t >= 2) & (t < n + 2))
        def _():
            wait_f_store(t % 2)

        @pl.when(last & (t >= 2) & (t < n + 2))
        def _():
            local(of.at[(t - 2) % NF], y.at[0], y_loc.at[(t - 2) % NF]).wait()

            @pl.when(t - 2 < YC)
            def _():
                send_y(t - 2)
        for at, m in LATE_Y.items():
            @pl.when(last & (t == at))
            def _(m=m):
                send_y(m)

        @pl.when((t >= w) & (t - w < n))
        def _():
            backward(t - w)

        @pl.when((w > 1) & (t - w + 1 >= 0) & (t - w + 1 < n))
        def _():
            local(gps.at[t - w + 1], gp.at[2], pf_sem).start()

        @pl.when(t < n)
        def _():
            forward(t)

        @pl.when((t >= t0) & (t < t0 + n_grp))
        def _():
            w_group(t - t0)

        @pl.when(t == t0 - 1)
        def _():
            w_load(0)

        mp = t - off_p

        @pl.when((mp >= 0) & (mp < YC) & (mp % 2 == par_y))
        def _():
            pass_y(mp)
        ml = t - (n + w + 2) + YC

        @pl.when(relay_y & (ml >= YC) & (ml < n) & (ml % 2 == par_y))
        def _():
            pass_y(ml)
        ms = t - off_s

        @pl.when((ms >= 0) & (ms < YC) & (ms % 2 != par_y))
        def _():
            pass_y(ms)
        mx = t - w - lag_x

        @pl.when(relay_x & (mx >= 0) & (mx < n))
        def _():
            pass_x(mx)
        return c
    lax.fori_loop(0, ticks, tick, 0)

    x0 = jnp.where(relay_x, jnp.clip(ticks - w - lag_x, 0, n), jnp.where(first, n, 0))

    def left_p(m):
        at = jnp.where(m < YC, m + off_p, jnp.where(relay_y, n + w + 2 + m - YC, 999))
        return (m % 2 == par_y) & (at >= ticks)

    def left_s(m):
        at = jnp.where(m < YC, m + off_s, 999)
        return (m % 2 != par_y) & (at >= ticks)

    def rest_p(m, c):
        @pl.when(left_p(m) | ((s == 1) & left_s(m)))
        def _():
            pass_y(m)
        return c

    def rest_s(m, c):
        @pl.when(left_s(m) & (s != 1))
        def _():
            pass_y(m)
        return c

    def rest_x(m, c):
        pass_x(m)
        return c
    early = jnp.where(relay_y, 0, n)
    late = jnp.where(relay_y | last, n, 0)
    lax.fori_loop(early, n, rest_p, 0)
    lax.fori_loop(early, n, rest_s, 0)
    lax.fori_loop(x0, n, rest_x, 0)
    lax.fori_loop(late, n, rest_p, 0)
    lax.fori_loop(late, n, rest_s, 0)

    @pl.when(jnp.logical_not(last))
    def _():
        for m in range(n - NF, n):
            wait_f_send(m % NF)
    for m in (n - 2, n - 1):
        wait_b_send(m % 2)
        local(gp.at[m % 2], gps.at[0], wo_sem.at[m % 2]).wait()
    local(dz, dzs.at[0], dz_sem).wait()
    local(h_all, hs, hs_sem).wait()
    local(g_all, gs, gs_sem).wait()

    def done(m, c):
        @pl.when(last)
        def _():
            for k in range(2):
                remote(y.at[m], y.at[m], y_send.at[k, m], y_recv.at[m], 6).wait_send()

        @pl.when(relay_y)
        def _():
            remote(y.at[m], y.at[m], yr_send.at[0, m], y_recv.at[m], s - 1).wait_send()

        @pl.when(second_y(m))
        def _():
            remote(y.at[m], y.at[m], yr_send.at[1, m], y_recv.at[m], next_y(m)).wait_send()

        @pl.when(relay_x)
        def _():
            remote(dx.at[m], dx.at[m], xr_send.at[0, m], x_recv.at[m], s + 1).wait_send()

        @pl.when(s == 2)
        def _():
            remote(dx.at[m], dx.at[m], xr_send.at[1, m], x_recv.at[m], 6).wait_send()
        return c
    lax.fori_loop(0, n, done, 0)


def _run_pipe(n_st, x, g, w1, w2):
    n, b, d = x.shape
    f = w1.shape[1]
    act = jax.ShapeDtypeStruct((n, b, d), BF)
    wide = jax.ShapeDtypeStruct((n, b, f), BF)
    anyspec = pl.BlockSpec(memory_space=pl.ANY)
    dma = pltpu.SemaphoreType.DMA
    return pl.pallas_call(
        functools.partial(_pipe, n, n_st),
        out_shape=(act, act, act, act, wide, wide, jax.ShapeDtypeStruct((n, b, f), F32),
                   jax.ShapeDtypeStruct((d, f), F32), jax.ShapeDtypeStruct((f, d), F32)),
        in_specs=[anyspec] * 4,
        out_specs=(anyspec,) * 9,
        scratch_shapes=[
            pltpu.VMEM((d, f), BF), pltpu.VMEM((f, d), BF),
            pltpu.VMEM((n, b, d), BF), pltpu.VMEM((n, b, d), BF),
            pltpu.VMEM((4, b, f), BF), pltpu.VMEM((3, b, f), F32), pltpu.VMEM((b, f), BF),
            pltpu.VMEM((NF, b, d), BF), pltpu.VMEM((2, b, d), BF),
            dma((2,)), dma((n,)), dma((n,)), dma((n,)), dma((n,)), dma, dma,
            dma((2,)), dma((2,)), dma, dma, dma((NF,)), dma((2,)),
            dma((NF,)), dma((2, n)), dma((2,)), dma((3, 2)), dma((2, n)), dma((2, n)),
            dma((2,)), dma((2,)), dma((2,)),
        ],
        compiler_params=pltpu.CompilerParams(has_side_effects=True, vmem_limit_bytes=67043328),
    )(x, g, w1, w2)


def _finish(u, dz, h, g, p1, p2, y, dx, o1, o2, yo, dxo):
    o2[...] = p2[...] + lax.dot_general(u[...], g[...], TN, preferred_element_type=F32)
    o1[...] = p1[...] + lax.dot_general(h[...], dz[...], TN, preferred_element_type=F32)
    yo[...] = y[...]
    dxo[...] = dx[...]


def _run_finish(us, dzs, hs, gs, p1, p2, y, dx):
    n, b, d = y.shape
    f = us.shape[1]
    k = (n - KB) * b
    steps = f // FT
    m = n // steps
    one = pl.Buffered(1)
    act = pl.BlockSpec((m, b, d), lambda j: (j, 0, 0))
    col = pl.BlockSpec((d, FT), lambda j: (0, j))
    row = pl.BlockSpec((FT, d), lambda j: (j, 0))
    tok = pl.BlockSpec((k, FT), lambda j: (1, j))
    all_d = pl.BlockSpec((k, d), lambda j: (1, 0), pipeline_mode=one)
    return pl.pallas_call(
        _finish,
        grid=(steps,),
        out_shape=(jax.ShapeDtypeStruct((d, f), F32), jax.ShapeDtypeStruct((f, d), F32),
                   jax.ShapeDtypeStruct((n, b, d), BF), jax.ShapeDtypeStruct((n, b, d), BF)),
        in_specs=[tok, tok, all_d, all_d, col, row, act, act],
        out_specs=[col, row, act, act],
        compiler_params=pltpu.CompilerParams(vmem_limit_bytes=63 * 1024 * 1024),
    )(us, dzs, hs, gs, p1, p2, y, dx)


def solution(mesh):
    n_st = mesh.shape['stage']

    def body(x, g, w1, w2):
        n, b, d = x.shape
        f = w1.shape[2]
        y, dx, hs, gs, us, dzs, _, p1, p2 = _run_pipe(n_st, x, g, w1[0], w2[0])
        dw1, dw2, y, dx = _run_finish(us.reshape(n * b, f), dzs.reshape(n * b, f), hs.reshape(n * b, d),
                                      gs.reshape(n * b, d), p1, p2, y, dx)
        return y, dx, dw1[None], dw2[None]

    return jax.shard_map(body, mesh=mesh,
                         in_specs=(P('data'), P('data'), P('stage'), P('stage')),
                         out_specs=(P('data'), P('data'), P(('data', 'stage')), P(('data', 'stage'))),
                         check_vma=False)
```

time: 447 us -> 401 us (0.90)
  the two profiles are of different devices: /device:TPU:15 before, /device:TPU:10 now
where the time goes in v2:
time: 401 us
  Pallas kernels  400 us (100%)
    pallas_call x1, Pallas kernels, _run_pipe(): pl.pallas_call(functools.partial(_pipe, n, n_st), out_shape=(act, act, ac...  344 us
    pallas_call x1, Pallas kernels, _run_finish(): pl.pallas_call(_finish, grid=(steps,), out_shape=(jax.ShapeDtypeStruct((d...  56 us

profile of v2, /device:TPU:10, one launch (start us, length us, event | category | flops | bytes accessed | tf_op | source)
XLA Modules:
  0.0 400.7 jit_solution(1911481379442550154)
XLA Ops:
  0.6 344.0 %shard_map.75 = (bf16[16,256,1024]{2,1,0:T(8,128)(2,1)}, bf16[16,256,1024]{2,1,0:T(8,128)(2,1)}, bf16[16,256,1024]{2,1,0:T(8,128)(2,1)}, bf16[16,256,1024]{2,1,0...) custom-call(bf16[16,256,1024]{2,1,0:T(8,128)(2,1)} %x.1, ...), custom_call_target="tpu_custom_call" | custom-call | tf_op jit(solution)/shard_map/pallas_call | solution.py:393
  344.6 56.0 %shard_map.76 = (f32[1024,4096]{1,0:T(8,128)}, f32[4096,1024]{1,0:T(8,128)}, bf16[16,256,1024]{2,1,0:T(8,128)(2,1)}, bf16[16,256,1024]{2,1,0:T(8,128)(2,1)}) custom-call(bf16[4096,4096]{1,0:T(8,128)(2,1)} %bitcast.8, bf16[4096,4096]{1,0:T(8,128)(2,1)} %bitcast.9, bf16[4096,1024]{1,0:T(8,128)(2,1)} %bitcast.10, bf16[4096,1024]{1,0:T(8,128)(2,1)} %bitcast.11, ...), custom_call_target="tpu_custom_call" | custom-call | tf_op jit(solution)/shard_map/pallas_call | solution.py:432

commit v3 on v2

--- a/solution.py
+++ b/solution.py
@@ -70,6 +70,11 @@
         local(x.at[0], h_all.at[0], h_recv.at[0]).start()
     local(w1h, w1, w_sem.at[0]).start()
     local(w2h, w2, w_sem.at[1]).start()
+    barrier = pltpu.get_barrier_semaphore()
+    for k in range(1, n_st):
+        pl.semaphore_signal(barrier, inc=1, device_id={'stage': lax.rem(s + k, n_st)},
+                            device_id_type=pl.DeviceIdType.MESH)
+    pl.semaphore_wait(barrier, n_st - 1)
 
     @pl.when(last)
     def _():
@@ -248,7 +253,8 @@
                   p1.at[pl.ds(b * q, b), pl.ds(pl.multiple_of(i * FT, FT), FT)], wo_sem.at[sl]).start()
 
     t0 = _pick(s, T_W)
-    ticks = jnp.maximum(jnp.maximum(n + w, t0 + n_grp), n + 2)
+    gap = jnp.where(s <= 1, 3, 0)
+    ticks = jnp.maximum(jnp.maximum(n + w, t0 + n_grp + gap), n + 2)
 
     def send_y(m):
         remote(y.at[m], y.at[m], y_send.at[0, m], y_recv.at[m], 6).start()
@@ -283,9 +289,12 @@
         def _():
             forward(t)
 
-        @pl.when((t >= t0) & (t < t0 + n_grp))
-        def _():
-            w_group(t - t0)
+        k = t - t0
+        grp = jnp.where(k < 4, k, k - gap)
+
+        @pl.when((k >= 0) & ((k < 4) | (k - gap >= 4)) & (grp < n_grp))
+        def _():
+            w_group(grp)
 
         @pl.when(t == t0 - 1)
         def _():
@@ -406,7 +415,7 @@
             dma((NF,)), dma((2, n)), dma((2,)), dma((3, 2)), dma((2, n)), dma((2, n)),
             dma((2,)), dma((2,)), dma((2,)),
         ],
-        compiler_params=pltpu.CompilerParams(has_side_effects=True, vmem_limit_bytes=67043328),
+        compiler_params=pltpu.CompilerParams(has_side_effects=True, collective_id=0, vmem_limit_bytes=67043328),
     )(x, g, w1, w2)
 
 

time: 401 us -> 400 us (level)
  the two profiles are of different devices: /device:TPU:10 before, /device:TPU:0 now
where the time goes in v3:
time: 400 us; the launch traced here: 393 us
  Pallas kernels  392 us (98%)
    pallas_call x1, Pallas kernels, _run_pipe(): pl.pallas_call(functools.partial(_pipe, n, n_st), out_shape=(act, act, ac...  336 us
    pallas_call x1, Pallas kernels, _run_finish(): pl.pallas_call(_finish, grid=(steps,), out_shape=(jax.ShapeDtypeStruct((d...  56 us

profile of v3, /device:TPU:0, one launch (start us, length us, event | category | flops | bytes accessed | tf_op | source)
XLA Modules:
  0.0 392.6 jit_solution(12381886959249758258)
XLA Ops:
  0.6 335.9 %shard_map.75 = (bf16[16,256,1024]{2,1,0:T(8,128)(2,1)}, bf16[16,256,1024]{2,1,0:T(8,128)(2,1)}, bf16[16,256,1024]{2,1,0:T(8,128)(2,1)}, bf16[16,256,1024]{2,1,0...) custom-call(bf16[16,256,1024]{2,1,0:T(8,128)(2,1)} %x.1, ...), custom_call_target="tpu_custom_call" | custom-call | tf_op jit(solution)/shard_map/pallas_call | solution.py:402
  336.6 56.0 %shard_map.76 = (f32[1024,4096]{1,0:T(8,128)}, f32[4096,1024]{1,0:T(8,128)}, bf16[16,256,1024]{2,1,0:T(8,128)(2,1)}, bf16[16,256,1024]{2,1,0:T(8,128)(2,1)}) custom-call(bf16[4096,4096]{1,0:T(8,128)(2,1)} %bitcast.8, bf16[4096,4096]{1,0:T(8,128)(2,1)} %bitcast.9, bf16[4096,1024]{1,0:T(8,128)(2,1)} %bitcast.10, bf16[4096,1024]{1,0:T(8,128)(2,1)} %bitcast.11, ...), custom_call_target="tpu_custom_call" | custom-call | tf_op jit(solution)/shard_map/pallas_call | solution.py:441
